TPU v7x, 32 devices: a whole 2x2x4 slice. The times are simulated.
32 devices in a mesh: dp: 8 (over z, y), tensor: 4 (over x, core).
Axes of the slice: x: 2, y: 2, z: 4, core: 2. Of those that a mesh axis runs over, the one named last changes fastest.
Arguments:
- inputs: bfloat16 [26656, 768], P('dp'), may hold values from -6 to 6
- cotangent: bfloat16 [26656, 768], P('dp'), may hold values from -6 to 6
- master_inward: float32 [3, 768, 768], P(None, 'dp', 'tensor'), may hold values from -0.28867513 to 0.28867513
- first_inward: float32 [3, 768, 768], P(None, 'dp', 'tensor'), may hold values from -512 to 512
- second_inward: float32 [3, 768, 768], P(None, 'dp', 'tensor'), may hold values from 3332 to 53312
- master_outward: float32 [768, 768], P('tensor', 'dp'), may hold values from -0.8164966 to 0.8164966
- first_outward: float32 [768, 768], P('tensor', 'dp'), may hold values from -320 to 320
- second_outward: float32 [768, 768], P('tensor', 'dp'), may hold values from 1332.8 to 21324.8
- master_widening: float32 [768, 3072], P('dp', 'tensor'), may hold values from -0.28867513 to 0.28867513
- first_widening: float32 [768, 3072], P('dp', 'tensor'), may hold values from -320 to 320
- second_widening: float32 [768, 3072], P('dp', 'tensor'), may hold values from 1332.8 to 21324.8
- master_narrowing: float32 [3072, 768], P('tensor', 'dp'), may hold values from -0.14433757 to 0.14433757
- first_narrowing: float32 [3072, 768], P('tensor', 'dp'), may hold values from -640 to 640
- second_narrowing: float32 [3072, 768], P('tensor', 'dp'), may hold values from 5331.2 to 85299.2
- master_scaling: float32 [768], P('dp'), may hold values from 0.5 to 1.5
- first_scaling: float32 [768], P('dp'), may hold values from -1024 to 1024
- second_scaling: float32 [768], P('dp'), may hold values from 13328 to 213248
Outputs:
- output: bfloat16 [26656, 768], P(('dp', 'tensor'))
- input_grad: bfloat16 [26656, 768], P('dp')
- moment_inward: float32 [3, 768, 768], P(None, 'dp', 'tensor')
- square_inward: float32 [3, 768, 768], P(None, 'dp', 'tensor')
- weight_inward: float32 [3, 768, 768], P(None, 'dp', 'tensor')
- bfloat_inward: bfloat16 [3, 768, 768], P(None, 'dp', 'tensor')
- moment_outward: float32 [768, 768], P('tensor', 'dp')
- square_outward: float32 [768, 768], P('tensor', 'dp')
- weight_outward: float32 [768, 768], P('tensor', 'dp')
- bfloat_outward: bfloat16 [768, 768], P('tensor', 'dp')
- moment_widening: float32 [768, 3072], P('dp', 'tensor')
- square_widening: float32 [768, 3072], P('dp', 'tensor')
- weight_widening: float32 [768, 3072], P('dp', 'tensor')
- bfloat_widening: bfloat16 [768, 3072], P('dp', 'tensor')
- moment_narrowing: float32 [3072, 768], P('tensor', 'dp')
- square_narrowing: float32 [3072, 768], P('tensor', 'dp')
- weight_narrowing: float32 [3072, 768], P('tensor', 'dp')
- bfloat_narrowing: bfloat16 [3072, 768], P('tensor', 'dp')
- moment_scaling: float32 [768], P('dp')
- square_scaling: float32 [768], P('dp')
- weight_scaling: float32 [768], P('dp')
- bfloat_scaling: bfloat16 [768], P('dp')
- trust_norms: float32 [5, 2], replicated
All inputs are finite; a program needn't handle non-finite values.
Results may differ from a plain program's by a relative error of at most 0.012.
The roundings to bfloat16 on the way count: a program that leaves them out, or rounds other values in their place, can miss the bound.
Values may be sent and summed in bfloat16 or wider, within the bound.
A program may use at most 192 MiB of HBM per device.

v0:
```python
import jax
import jax.numpy as jnp
from jax import lax
from jax.sharding import PartitionSpec as P

HEAD_DIM = 64
SEQ = 196
STEP = 5
norm_eps = 1e-06
beta_one = 0.5
beta_two = 0.5
lamb_eps = 1e-06
weight_decay = 0.01
learn_rate = 0.5


def lamb_parts(master, first, second, grad):
    moment = beta_one * first + (1.0 - beta_one) * grad
    square = beta_two * second + (1.0 - beta_two) * grad * grad
    update = (
        moment / (1.0 - beta_one**STEP) / (jnp.sqrt(square / (1.0 - beta_two**STEP)) + lamb_eps)
        + weight_decay * master
    )
    return (moment, square, update)


def gelu_tanh(values):
    return jax.nn.gelu(values, approximate=True)


def local(
    inputs,
    cotangent,
    master_inward,
    first_inward,
    second_inward,
    master_outward,
    first_outward,
    second_outward,
    master_widening,
    first_widening,
    second_widening,
    master_narrowing,
    first_narrowing,
    second_narrowing,
    master_scaling,
    first_scaling,
    second_scaling,
):
    inward, outward, widening, narrowing, scaling = (
        lax.all_gather(master_inward.astype(jnp.bfloat16), "dp", axis=1, tiled=True),
        lax.all_gather(master_outward.astype(jnp.bfloat16), "dp", axis=1, tiled=True),
        lax.all_gather(master_widening.astype(jnp.bfloat16), "dp", axis=0, tiled=True),
        lax.all_gather(master_narrowing.astype(jnp.bfloat16), "dp", axis=1, tiled=True),
        lax.all_gather(master_scaling.astype(jnp.bfloat16), "dp", axis=0, tiled=True),
    )
    floats_in = inputs.astype(jnp.float32)
    rows_here = floats_in.shape[0]
    images = rows_here // SEQ
    heads_here = inward.shape[2] // HEAD_DIM
    factor = HEAD_DIM ** (-0.5)
    centred = floats_in - jnp.mean(floats_in, axis=1, keepdims=True)
    inv_std = lax.rsqrt(jnp.mean(centred * centred, axis=1, keepdims=True) + norm_eps)
    unit_rows = centred * inv_std
    gain_rows = scaling.astype(jnp.float32)
    normed = (unit_rows * gain_rows).astype(jnp.bfloat16)
    projected = jnp.einsum(
        "rd,tde->tre", normed, inward, preferred_element_type=jnp.float32
    ).astype(jnp.bfloat16)
    blocks = projected.reshape(3, images, SEQ, heads_here, HEAD_DIM)
    query_rows, key_rows, value_rows = (blocks[0], blocks[1], blocks[2])
    scores = (
        jnp.einsum("bqhd,bkhd->bhqk", query_rows, key_rows, preferred_element_type=jnp.float32)
        * factor
    )
    peak = jnp.max(scores, axis=-1, keepdims=True)
    log_total = peak + jnp.log(jnp.sum(jnp.exp(scores - peak), axis=-1, keepdims=True))
    probs_low = jnp.exp(scores - log_total).astype(jnp.bfloat16)
    attended = jnp.einsum(
        "bhqk,bkhd->bqhd", probs_low, value_rows, preferred_element_type=jnp.float32
    )
    attended = attended.astype(jnp.bfloat16).reshape(rows_here, heads_here * HEAD_DIM)
    upper = jnp.dot(normed, widening, preferred_element_type=jnp.float32)
    hidden = gelu_tanh(upper).astype(jnp.bfloat16)
    partial_sum = jnp.dot(attended, outward, preferred_element_type=jnp.float32) + jnp.dot(
        hidden, narrowing, preferred_element_type=jnp.float32
    )
    share = rows_here // lax.axis_size("tensor")
    start = lax.axis_index("tensor") * share
    total = lax.psum(partial_sum.astype(jnp.bfloat16), "tensor").astype(jnp.float32)
    mixed = lax.dynamic_slice_in_dim(floats_in, start, share, 0) + lax.dynamic_slice_in_dim(
        total, start, share, 0
    )
    output = mixed.astype(jnp.bfloat16)
    d_attended = jnp.einsum(
        "rd,ed->re", cotangent, outward, preferred_element_type=jnp.float32
    ).astype(jnp.bfloat16)
    grad_outward = jnp.einsum("re,rd->ed", attended, cotangent, preferred_element_type=jnp.float32)
    d_hidden = jnp.einsum("rd,fd->rf", cotangent, narrowing, preferred_element_type=jnp.float32)
    grad_narrowing = jnp.einsum("rf,rd->fd", hidden, cotangent, preferred_element_type=jnp.float32)
    gelu_value, gelu_pull = jax.vjp(gelu_tanh, upper)
    d_upper = gelu_pull(d_hidden)[0].astype(jnp.bfloat16)
    grad_widening = jnp.einsum("rd,rf->df", normed, d_upper, preferred_element_type=jnp.float32)
    back_sum = jnp.einsum("rf,df->rd", d_upper, widening, preferred_element_type=jnp.float32)
    d_att_blocks = d_attended.reshape(images, SEQ, heads_here, HEAD_DIM)
    rescored = (
        jnp.einsum("bqhd,bkhd->bhqk", query_rows, key_rows, preferred_element_type=jnp.float32)
        * factor
    )
    probs_full = jnp.exp(rescored - log_total)
    probs_again = probs_full.astype(jnp.bfloat16)
    d_probs = jnp.einsum(
        "bqhd,bkhd->bhqk", d_att_blocks, value_rows, preferred_element_type=jnp.float32
    )
    d_value = jnp.einsum(
        "bhqk,bqhd->bkhd", probs_again, d_att_blocks, preferred_element_type=jnp.float32
    ).astype(jnp.bfloat16)
    inner = jnp.sum(probs_full * d_probs, axis=-1, keepdims=True)
    d_scores = (probs_full * (d_probs - inner)).astype(jnp.bfloat16)
    d_query = (
        jnp.einsum("bhqk,bkhd->bqhd", d_scores, key_rows, preferred_element_type=jnp.float32)
        * factor
    ).astype(jnp.bfloat16)
    d_key = (
        jnp.einsum("bhqk,bqhd->bkhd", d_scores, query_rows, preferred_element_type=jnp.float32)
        * factor
    ).astype(jnp.bfloat16)
    d_projected = jnp.stack([d_query, d_key, d_value]).reshape(3, rows_here, heads_here * HEAD_DIM)
    grad_inward = jnp.einsum("rd,tre->tde", normed, d_projected, preferred_element_type=jnp.float32)
    back_sum = back_sum + jnp.einsum(
        "tre,tde->rd", d_projected, inward, preferred_element_type=jnp.float32
    )
    d_normed = lax.psum(back_sum.astype(jnp.bfloat16), "tensor").astype(jnp.float32)
    grad_scaling = jnp.sum(d_normed * unit_rows, axis=0)
    d_unit = d_normed * gain_rows
    d_floats = inv_std * (
        d_unit
        - jnp.mean(d_unit, axis=1, keepdims=True)
        - unit_rows * jnp.mean(d_unit * unit_rows, axis=1, keepdims=True)
    )
    input_grad = (cotangent.astype(jnp.float32) + d_floats).astype(jnp.bfloat16)
    grad_inward, grad_outward, grad_widening, grad_narrowing, grad_scaling = (
        lax.psum_scatter(grad_inward, "dp", scatter_dimension=1, tiled=True),
        lax.psum_scatter(grad_outward, "dp", scatter_dimension=1, tiled=True),
        lax.psum_scatter(grad_widening, "dp", scatter_dimension=0, tiled=True),
        lax.psum_scatter(grad_narrowing, "dp", scatter_dimension=1, tiled=True),
        lax.psum_scatter(grad_scaling, "dp", scatter_dimension=0, tiled=True),
    )
    part_in = lamb_parts(master_inward, first_inward, second_inward, grad_inward)
    part_out = lamb_parts(master_outward, first_outward, second_outward, grad_outward)
    part_wide = lamb_parts(master_widening, first_widening, second_widening, grad_widening)
    part_narrow = lamb_parts(master_narrowing, first_narrowing, second_narrowing, grad_narrowing)
    part_scale = lamb_parts(master_scaling, first_scaling, second_scaling, grad_scaling)
    replicas = 1.0 / lax.axis_size("tensor")
    local_sums = jnp.stack(
        [
            jnp.stack([jnp.sum(master_inward * master_inward), jnp.sum(part_in[2] * part_in[2])]),
            jnp.stack(
                [jnp.sum(master_outward * master_outward), jnp.sum(part_out[2] * part_out[2])]
            ),
            jnp.stack(
                [jnp.sum(master_widening * master_widening), jnp.sum(part_wide[2] * part_wide[2])]
            ),
            jnp.stack(
                [
                    jnp.sum(master_narrowing * master_narrowing),
                    jnp.sum(part_narrow[2] * part_narrow[2]),
                ]
            ),
            jnp.stack(
                [jnp.sum(master_scaling * master_scaling), jnp.sum(part_scale[2] * part_scale[2])]
            )
            * replicas,
        ]
    )
    trust_norms = jnp.sqrt(lax.psum(local_sums, ("dp", "tensor")))
    fresh_in = master_inward - learn_rate * (trust_norms[0, 0] / trust_norms[0, 1]) * part_in[2]
    fresh_out = master_outward - learn_rate * (trust_norms[1, 0] / trust_norms[1, 1]) * part_out[2]
    fresh_wide = (
        master_widening - learn_rate * (trust_norms[2, 0] / trust_norms[2, 1]) * part_wide[2]
    )
    fresh_narrow = (
        master_narrowing - learn_rate * (trust_norms[3, 0] / trust_norms[3, 1]) * part_narrow[2]
    )
    fresh_scale = (
        master_scaling - learn_rate * (trust_norms[4, 0] / trust_norms[4, 1]) * part_scale[2]
    )
    return (
        output,
        input_grad,
        part_in[0],
        part_in[1],
        fresh_in,
        fresh_in.astype(jnp.bfloat16),
        part_out[0],
        part_out[1],
        fresh_out,
        fresh_out.astype(jnp.bfloat16),
        part_wide[0],
        part_wide[1],
        fresh_wide,
        fresh_wide.astype(jnp.bfloat16),
        part_narrow[0],
        part_narrow[1],
        fresh_narrow,
        fresh_narrow.astype(jnp.bfloat16),
        part_scale[0],
        part_scale[1],
        fresh_scale,
        fresh_scale.astype(jnp.bfloat16),
        trust_norms,
    )


def solution(mesh):
    in_specs = (
        P("dp", None),
        P("dp", None),
        P(None, "dp", "tensor"),
        P(None, "dp", "tensor"),
        P(None, "dp", "tensor"),
        P("tensor", "dp"),
        P("tensor", "dp"),
        P("tensor", "dp"),
        P("dp", "tensor"),
        P("dp", "tensor"),
        P("dp", "tensor"),
        P("tensor", "dp"),
        P("tensor", "dp"),
        P("tensor", "dp"),
        P("dp"),
        P("dp"),
        P("dp"),
    )
    out_specs = (
        P(("dp", "tensor"), None),
        P("dp", None),
        P(None, "dp", "tensor"),
        P(None, "dp", "tensor"),
        P(None, "dp", "tensor"),
        P(None, "dp", "tensor"),
        P("tensor", "dp"),
        P("tensor", "dp"),
        P("tensor", "dp"),
        P("tensor", "dp"),
        P("dp", "tensor"),
        P("dp", "tensor"),
        P("dp", "tensor"),
        P("dp", "tensor"),
        P("tensor", "dp"),
        P("tensor", "dp"),
        P("tensor", "dp"),
        P("tensor", "dp"),
        P("dp"),
        P("dp"),
        P("dp"),
        P("dp"),
        P(),
    )
    return jax.shard_map(local, mesh=mesh, in_specs=in_specs, out_specs=out_specs, check_vma=False)
```

profile of v0, /device:TPU:10, one launch (start us, length us, event | category | flops | bytes accessed | tf_op | source)
XLA Modules:
  0.0 707.1 jit_solution(8922916075300123028)
XLA Ops:
  7.3 1.6 convert_element_type.117
  9.0 3.2 convert_reduce_fusion
  14.3 19.0 %all-reduce = bf16[768]{0:T(1024)(128)(2,1)S(1)} all-reduce(bf16[768]{0:T(1024)(128)(2,1)S(1)} %dynamic-update-slice), channel_id=1, replica_groups=mesh['dp'=8,'tensor'=4] {'dp'}, use_global_device_ids=true, to_apply=%add | all-reduce | flops 768 | bytes 3072
  33.3 4.1 multiply_reduce_fusion.1
  38.0 6.7 multiply_convert_fusion.2
  44.7 7.6 %all-gather.3.cloned.1.call-done = bf16[768,768]{1,0:T(8,128)(2,1)} async-done(((bf16[96,768]{1,0:T(8,128)(2,1)}), bf16[768,768]{1,0:T(8,128)(2,1)}) %all-gather.3.cloned.1.call-update) | async-done | bytes 1179664 | tf_op jit(solution)/shard_map/all_gather | solution.py:53
  52.3 6.5 fusion.62
  58.9 3.9 copy-done.47
  62.8 9.5 %fusion.46 = f32[768,768]{0,1:T(8,128)} fusion(bf16[3332,768]{1,0:T(8,128)(2,1)} %param.18, f32[3332,768]{1,0:T(8,128)S(1)} %fusion.62), kind=kOutput, calls=%fused_computation.109 | convolution fusion | flops 3953617920 | bytes 17713152 | tf_op jit(solution)/shard_map/rf,rd->fd/dot_general | solution.py:100
  73.2 40.9 %all_gather.16 = bf16[3,768,192]{2,0,1:T(4,128)(2,1)S(1)} all-gather(bf16[3,96,192]{2,0,1:T(4,128)(2,1)S(1)} %copy.122), channel_id=1, replica_groups=mesh['dp'=8,'tensor'=4] {'dp'}, dimensions={1}, use_global_device_ids=true | all-gather | bytes 995328 | tf_op jit(solution)/shard_map/all_gather | solution.py:51
  115.0 5.9 fusion.61
  121.3 1.3 fusion.58
  122.7 3.8 squeeze.7
  126.5 3.8 squeeze.8
  130.3 4.2 squeeze.6
  134.5 9.5 %multiply_reduce_fusion.2 = (f32[17,3,196]{2,1,0:T(4,128)S(1)}, f32[17,3,196,196]{2,3,1,0:T(8,128)}) fusion(bf16[17,196,3,64]{1,0,3,2:T(8,128)(2,1)} %squeeze.8, bf16[17,196,3,64]{1,0,3,2:T(8,128)(2,1)} %squeeze.7), kind=kOutput, calls=%fused_computation.31 | convolution fusion | flops 254688080 | bytes 10435824 | tf_op jit(solution)/shard_map/bqhd,bkhd->bhqk/dot_general | solution.py:73
  144.0 8.9 %reduce-scatter.11.cloned.1.call-done = f32[768,96]{0,1:T(8,128)} async-done(((f32[768,768]{0,1:T(8,128)}), f32[768,96]{0,1:T(8,128)}) %reduce-scatter.11.cloned.1.call-update) | async-done | bytes 294928 | tf_op jit(solution)/shard_map/reduce_scatter | solution.py:146
  152.8 2.6 multiply_reduce_fusion.4
  155.7 6.3 exponential_reduce_fusion
  162.7 2.1 fusion.23
  165.9 2.6 reshape.143
  168.5 6.0 convolution_bitcast_fusion
  174.6 30.0 %all_gather.17 = bf16[192,768]{0,1:T(8,128)(2,1)S(1)} all-gather(bf16[192,96]{0,1:T(8,128)(2,1)S(1)} %copy.129), channel_id=1, replica_groups=mesh['dp'=8,'tensor'=4] {'dp'}, dimensions={1}, use_global_device_ids=true | all-gather | bytes 331776 | tf_op jit(solution)/shard_map/all_gather | solution.py:52
  205.4 4.2 convolution_convert_fusion
  209.7 4.3 reshape.144
  214.0 12.7 %multiply_reduce_fusion = (f32[17,3,196]{2,1,0:T(4,128)S(1)}, f32[17,3,196,196]{2,3,1,0:T(8,128)}) fusion(f32[17,3,196,196]{2,3,1,0:T(8,128)} %get-tuple-element.170, f32[17,3,196]{2,1,0:T(4,128)S(1)} %log_add_fusion, bf16[17,196,3,64]{1,0,3,2:T(8,128)(2,1)} %copy-done.1, bf16[17,196,3,64]{1,0,3,2:T(8,128)(2,1)} %reshape.144), kind=kOutput, calls=%fused_computation.8 | convolution fusion | flops 258606512 | bytes 18312672 | tf_op jit(solution)/shard_map/bqhd,bkhd->bhqk/dot_general | solution.py:112
  226.7 5.9 multiply_convert_fusion
  232.7 1.8 fusion.26
  234.5 2.2 fusion.25
  236.7 3.3 fusion.24
  240.9 2.6 stack.74
  243.6 2.5 copy.134
  246.0 2.8 stack.73
  248.8 2.5 constant_dynamic-update-slice_fusion.2
  251.3 2.5 copy.140
  253.8 2.6 stack.75
  256.4 2.5 constant_dynamic-update-slice_fusion.1
  258.9 2.5 constant_dynamic-update-slice_fusion
  261.4 8.3 %fusion.20 = f32[3,768,192]{1,2,0:T(8,128)} fusion(bf16[3,3332,192]{1,2,0:T(8,128)(2,1)} %constant_dynamic-update-slice_fusion, bf16[3332,768]{1,0:T(8,128)(2,1)} %multiply_convert_fusion.2), kind=kOutput, calls=%fused_computation.43 | convolution fusion | flops 2947940352 | bytes 10725888 | tf_op jit(solution)/shard_map/rd,tre->tde/dot_general | solution.py:129
  269.7 2.9 copy.158
  272.6 2.8 reshape.154
  275.5 12.9 %fusion.15 = bf16[3332,768]{1,0:T(8,128)(2,1)S(1)} fusion(f32[3332,768]{1,0:T(8,128)} %copy-done.47, bf16[3332,768]{1,0:T(8,128)(2,1)} %param.18, bf16[768,768]{0,1:T(8,128)(2,1)} %all-gather.5.cloned.1.call-done), kind=kOutput, calls=%fused_computation.23 | convolution fusion | flops 3981766656 | bytes 21651456 | tf_op jit(solution)/shard_map/rd,fd->rf/dot_general | solution.py:99
  288.5 2.2 copy-done.45
  290.7 8.6 %fusion.64 = f32[768,768]{1,0:T(8,128)} fusion(bf16[3332,768]{1,0:T(8,128)(2,1)} %multiply_convert_fusion.2, bf16[3332,768]{1,0:T(8,128)(2,1)S(1)} %fusion.15), kind=kOutput, calls=%fused_computation.122 | convolution fusion | flops 3930587136 | bytes 12595200 | tf_op jit(solution)/shard_map/rd,rf->df/dot_general | solution.py:103
  299.4 9.3 %fusion.47 = f32[3332,768]{1,0:T(8,128)S(1)} fusion(bf16[768,768]{0,1:T(8,128)(2,1)S(1)} %copy-done.44, f32[3332,768]{1,0:T(8,128)} %copy-done.47), kind=kOutput, calls=%fused_computation.110 | convolution fusion | flops 3953617920 | bytes 21651456 | tf_op jit(solution)/shard_map/dot_general | solution.py:85
  308.7 4.0 add_convert_fusion
  312.7 4.4 fusion.63
  317.2 6.6 fusion.16
  325.0 7.2 %convert_element_type.106 = f32[3332,768]{1,0:T(8,128)} convert(bf16[3332,768]{1,0:T(8,128)(2,1)} %param.17) | non-fusion elementwise | flops 2558976 | bytes 15353856 | tf_op jit(solution)/shard_map/convert_element_type | solution.py:57
  334.9 1.4 maximum_bitcast_fusion.1
  336.4 7.0 reduce-scatter.13.cloned.1.call-done
  345.5 1.4 maximum_bitcast_fusion
  347.9 1.4 maximum_bitcast_fusion.3
  349.3 66.2 %reduce-scatter.9.cloned.1.call-done = f32[96,768]{1,0:T(8,128)} async-done(((f32[768,768]{1,0:T(8,128)}), f32[96,768]{1,0:T(8,128)}) %reduce-scatter.9.cloned.1.call-update) | async-done | bytes 294928 | tf_op jit(solution)/shard_map/reduce_scatter | solution.py:145
  415.6 1.8 multiply_reduce_fusion.6
  417.4 1.4 maximum_bitcast_fusion.2
  418.8 182.2 %all-reduce.5.cloned.1.call-done = (bf16[3332,768]{1,0:T(8,128)(2,1)}, bf16[3332,768]{1,0:T(8,128)(2,1)}) async-done(((bf16[3332,768]{1,0:T(8,128)(2,1)}, bf16[3332,768]{1,0:T(8,128)(2,1)}), (bf16[3332,768]{1,0:T(8,128)(2,1)}, bf16[3332,768]{1,0:T(8,128)(2,1)})) %all-reduce.5.cloned.1.call-update) | async-done | bytes 10235920 | tf_op jit(solution)/shard_map/psum | solution.py:90
  601.0 7.5 %fusion.8 = (f32[768]{0:T(1024)S(1)}, f32[3332]{0:T(1024)S(1)}, f32[3332]{0:T(1024)S(1)}) fusion(bf16[3332,768]{1,0:T(8,128)(2,1)} %get-tuple-element.125, bf16[3332,768]{1,0:T(8,128)(2,1)} %param.17, f32[3332]{0:T(1024)S(1)} %copy-done.32, f32[3332]{0:T(1024)S(1)} %copy-done.22, f32[768]{0:T(1024)S(1)} %copy-done.36), kind=kLoop, calls=%fused_computation.16 | loop fusion | flops 25582328 | bytes 10295360 | tf_op jit(solution)/shard_map/reduce_sum | solution.py:134
  608.5 18.6 %all-reduce.1 = f32[768]{0:T(1024)S(1)} all-reduce(f32[768]{0:T(1024)S(1)} %get-tuple-element.115), channel_id=6, replica_groups=mesh['dp'=8,'tensor'=4] {'dp'}, use_global_device_ids=true, to_apply=%region_23.0.clone | all-reduce | flops 768 | bytes 6144
  627.2 1.2 multiply_reduce_fusion.11
  628.4 1.3 maximum_multiply_fusion
  630.7 42.7 %psum.23 = f32[5,2]{0,1:T(2,128)S(1)} all-reduce(f32[5,2]{0,1:T(2,128)S(1)} %stack.96), channel_id=1, replica_groups=mesh['dp'=8,'tensor'=4] {'dp','tensor'}, use_global_device_ids=true, to_apply=%region_25.0 | all-reduce | flops 10 | bytes 80 | tf_op jit(solution)/shard_map/psum | solution.py:176
  683.1 10.4 %fusion.6 = bf16[3332,768]{1,0:T(8,128)(2,1)} fusion(bf16[3332,768]{1,0:T(8,128)(2,1)} %get-tuple-element.125, bf16[3332,768]{1,0:T(8,128)(2,1)} %param.18, bf16[3332,768]{1,0:T(8,128)(2,1)} %param.17, f32[3332]{0:T(1024)S(1)} %get-tuple-element.173, f32[3332]{0:T(1024)S(1)} %get-tuple-element.174, f32[768]{0:T(1024)S(1)} %copy-done.36, ...), kind=kLoop, calls=%fused_computation.14 | loop fusion | flops 30707712 | bytes 20528192 | tf_op jit(solution)/shard_map/convert_element_type | solution.py:141
  696.1 3.7 add_convert_fusion.1
  (157 shorter events, 21.5 us)
Async XLA Ops:
  7.2 5.6 copy-start.40
  7.2 5.0 copy-start.38
  7.2 45.1 %all-gather.3.cloned.1.call-start = ((), (), s32[]{:S(2)}) async-start(), calls=%async_computation.4 | async-start | bytes 1327104 | tf_op jit(solution)/shard_map/all_gather | solution.py:53
  8.9 143.9 %reduce-scatter.11.cloned.1.call-start = ((), (), s32[]{:S(2)}) async-start(), calls=%async_computation.7 | async-start | bytes 2654208 | tf_op jit(solution)/shard_map/reduce_scatter | solution.py:146
  33.3 4.1 copy-start.35
  33.3 4.1 copy-start.21
  37.4 0.6 copy-start.31
  58.9 3.9 copy-start.47
  62.8 9.6 %copy-start.9 = (f32[3,96,192]{2,1,0:T(8,128)S(1)}, f32[3,96,192]{2,1,0:T(8,128)}, u32[]{:S(2)}) copy-start(f32[3,96,192]{2,1,0:T(8,128)} %param.19) | copy-start | bytes 663556
  72.3 203.2 %all-gather.5.cloned.1.call-start = ((), (), s32[]{:S(2)}) async-start(), calls=%async_computation.5 | async-start | bytes 1327104 | tf_op jit(solution)/shard_map/all_gather | solution.py:54
  115.0 5.9 copy-start.17
  134.4 27.6 %copy-start.1 = (bf16[17,196,3,64]{1,0,3,2:T(8,128)(2,1)}, bf16[17,196,3,64]{1,0,3,2:T(8,128)(2,1)S(1)}, u32[]{:S(2)}) copy-start(bf16[17,196,3,64]{1,0,3,2:T(8,128)(2,1)S(1)} %squeeze.6) | copy-start | bytes 3838468
  134.4 18.4 %copy-start.11 = (f32[768,96]{0,1:T(8,128)S(1)}, f32[768,96]{0,1:T(8,128)}, u32[]{:S(2)}) copy-start(f32[768,96]{0,1:T(8,128)} %param.28) | copy-start | bytes 884740
  134.5 18.4 %copy-start.25 = (f32[768,96]{0,1:T(8,128)S(1)}, f32[768,96]{0,1:T(8,128)}, u32[]{:S(2)}) copy-start(f32[768,96]{0,1:T(8,128)} %param.29) | copy-start | bytes 884740
  134.5 18.4 %copy-start.26 = (f32[768,96]{0,1:T(8,128)S(1)}, f32[768,96]{0,1:T(8,128)}, u32[]{:S(2)}) copy-start(f32[768,96]{0,1:T(8,128)} %param.30) | copy-start | bytes 884740
  155.5 177.8 %reduce-scatter.15.cloned.1.call-start = ((), (), s32[]{:S(2)}) async-start(), calls=%async_computation.9 | async-start | bytes 884736
  155.7 6.9 copy-start
  168.5 6.0 copy-start.19
  174.5 168.9 %reduce-scatter.13.cloned.1.call-start = ((), (), s32[]{:S(2)}) async-start(), calls=%async_computation.8 | async-start | bytes 2211840
  204.7 0.8 copy-start.6
  209.7 17.0 %slice-start = ((s8[10444800]{0:T(1024)(128)(4,1)}), s8[2056192]{0:T(1024)(128)(4,1)S(1)}, s32[]{:S(2)}) async-start(s8[10444800]{0:T(1024)(128)(4,1)} %bitcast.95), calls=%async_computation.11 | async-start | bytes 4112384
  214.0 12.7 %slice-start.1 = ((s8[10444800]{0:T(1024)(128)(4,1)}), s8[4194304]{0:T(1024)(128)(4,1)S(1)}, s32[]{:S(2)}) async-start(s8[10444800]{0:T(1024)(128)(4,1)} %bitcast.95), calls=%async_computation.12 | async-start | bytes 8388608
  214.0 12.7 %slice-start.2 = ((s8[10444800]{0:T(1024)(128)(4,1)}), s8[4194304]{0:T(1024)(128)(4,1)S(1)}, s32[]{:S(2)}) async-start(s8[10444800]{0:T(1024)(128)(4,1)} %bitcast.95), calls=%async_computation.13 | async-start | bytes 8388608
  226.7 5.9 copy-start.3
  232.7 1.8 copy-start.4
  234.5 2.2 copy-start.2
  275.5 140.1 %reduce-scatter.9.cloned.1.call-start = ((), (), s32[]{:S(2)}) async-start(), calls=%async_computation.6 | async-start | bytes 2654208 | tf_op jit(solution)/shard_map/reduce_scatter | solution.py:145
  288.4 2.2 copy-start.45
  290.7 8.7 %copy-start.44 = (bf16[768,768]{0,1:T(8,128)(2,1)S(1)}, bf16[768,768]{0,1:T(8,128)(2,1)}, u32[]{:S(2)}) copy-start(bf16[768,768]{0,1:T(8,128)(2,1)} %all-gather.5.cloned.1.call-done) | copy-start | bytes 3538948
  299.3 9.4 %copy-start.5 = (bf16[3332,192]{0,1:T(8,128)(2,1)S(1)}, bf16[3332,192]{0,1:T(8,128)(2,1)}, u32[]{:S(2)}) copy-start(bf16[3332,192]{0,1:T(8,128)(2,1)} %reshape.143) | copy-start | bytes 3838468
  299.3 9.4 %copy-start.7 = (bf16[192,768]{0,1:T(8,128)(2,1)S(1)}, bf16[192,768]{0,1:T(8,128)(2,1)}, u32[]{:S(2)}) copy-start(bf16[192,768]{0,1:T(8,128)(2,1)} %copy-done.6) | copy-start | bytes 884740
  299.3 301.7 %all-reduce.5.cloned.1.call-start = ((), (), s32[]{:S(2)}) async-start(), calls=%async_computation.10 | async-start | bytes 20496384 | tf_op jit(solution)/shard_map/psum | solution.py:90
  308.7 4.0 copy-start.43
  308.7 4.0 copy-start.46
  312.7 4.4 copy-start.18
  312.7 4.4 copy-start.20
  323.8 1.0 copy-start.10
  324.9 7.3 %copy-start.27 = (f32[3,96,192]{2,1,0:T(8,128)S(1)}, f32[3,96,192]{2,1,0:T(8,128)}, u32[]{:S(2)}) copy-start(f32[3,96,192]{2,1,0:T(8,128)} %param.20) | copy-start | bytes 663556
  324.9 7.5 %copy-start.28 = (f32[3,96,192]{2,1,0:T(8,128)S(1)}, f32[3,96,192]{2,1,0:T(8,128)}, u32[]{:S(2)}) copy-start(f32[3,96,192]{2,1,0:T(8,128)} %param.21) | copy-start | bytes 663556
  324.9 9.3 %copy-start.33 = (f32[192,96]{1,0:T(8,128)S(1)}, f32[192,96]{1,0:T(8,128)}, u32[]{:S(2)}) copy-start(f32[192,96]{1,0:T(8,128)} %param.23) | copy-start | bytes 221188
  325.0 9.3 %copy-start.34 = (f32[192,96]{1,0:T(8,128)S(1)}, f32[192,96]{1,0:T(8,128)}, u32[]{:S(2)}) copy-start(f32[192,96]{1,0:T(8,128)} %param.24) | copy-start | bytes 221188
  332.2 83.4 %copy-start.8 = (f32[96,768]{1,0:T(8,128)S(1)}, f32[96,768]{1,0:T(8,128)}, u32[]{:S(2)}) copy-start(f32[96,768]{1,0:T(8,128)} %param.25) | copy-start | bytes 884740
  332.2 83.4 %copy-start.29 = (f32[96,768]{1,0:T(8,128)S(1)}, f32[96,768]{1,0:T(8,128)}, u32[]{:S(2)}) copy-start(f32[96,768]{1,0:T(8,128)} %param.26) | copy-start | bytes 884740
  332.2 83.4 %copy-start.30 = (f32[96,768]{1,0:T(8,128)S(1)}, f32[96,768]{1,0:T(8,128)}, u32[]{:S(2)}) copy-start(f32[96,768]{1,0:T(8,128)} %param.27) | copy-start | bytes 884740
  332.2 268.8 %copy-start.22 = (f32[3332]{0:T(1024)S(1)}, f32[3332]{0:T(1024)}, u32[]{:S(2)}) copy-start(f32[3332]{0:T(1024)} %copy-done.21) | copy-start | bytes 39988
  332.2 268.8 %copy-start.32 = (f32[3332]{0:T(1024)S(1)}, f32[3332]{0:T(1024)}, u32[]{:S(2)}) copy-start(f32[3332]{0:T(1024)} %copy-done.31) | copy-start | bytes 39988
  332.2 268.8 %copy-start.36 = (f32[768]{0:T(1024)S(1)}, f32[768]{0:T(1024)}, u32[]{:S(2)}) copy-start(f32[768]{0:T(1024)} %copy-done.35) | copy-start | bytes 9220
  334.9 360.4 %copy-start.23 = (f32[192,96]{1,0:T(8,128)}, f32[192,96]{1,0:T(8,128)S(1)}, u32[]{:S(2)}) copy-start(f32[192,96]{1,0:T(8,128)S(1)} %get-tuple-element.144) | copy-start | bytes 221188
  334.9 360.4 %copy-start.24 = (f32[192,96]{1,0:T(8,128)}, f32[192,96]{1,0:T(8,128)S(1)}, u32[]{:S(2)}) copy-start(f32[192,96]{1,0:T(8,128)S(1)} %get-tuple-element.145) | copy-start | bytes 221188
  417.4 277.0 %copy-start.15 = (f32[96,768]{1,0:T(8,128)}, f32[96,768]{1,0:T(8,128)S(1)}, u32[]{:S(2)}) copy-start(f32[96,768]{1,0:T(8,128)S(1)} %get-tuple-element.142) | copy-start | bytes 884740
  417.4 277.0 %copy-start.16 = (f32[96,768]{1,0:T(8,128)}, f32[96,768]{1,0:T(8,128)S(1)}, u32[]{:S(2)}) copy-start(f32[96,768]{1,0:T(8,128)S(1)} %get-tuple-element.143) | copy-start | bytes 884740
  601.0 26.2 %copy-start.39 = (f32[96]{0:T(128)S(1)}, f32[96]{0:T(128)}, u32[]{:S(2)}) copy-start(f32[96]{0:T(128)} %param.31) | copy-start | bytes 1156
  601.0 26.2 %copy-start.41 = (f32[96]{0:T(128)S(1)}, f32[96]{0:T(128)}, u32[]{:S(2)}) copy-start(f32[96]{0:T(128)} %param.32) | copy-start | bytes 1156
  601.0 26.2 %copy-start.42 = (f32[96]{0:T(128)S(1)}, f32[96]{0:T(128)}, u32[]{:S(2)}) copy-start(f32[96]{0:T(128)} %param.33) | copy-start | bytes 1156
  673.4 20.1 %copy-start.37 = (f32[5,2]{0,1:T(2,128)}, f32[5,2]{0,1:T(2,128)S(1)}, u32[]{:S(2)}) copy-start(f32[5,2]{0,1:T(2,128)S(1)} %sqrt.23) | copy-start | bytes 124
  683.0 10.4 %copy-start.12 = (f32[768,96]{0,1:T(8,128)S(1)}, f32[768,96]{0,1:T(8,128)}, u32[]{:S(2)}) copy-start(f32[768,96]{0,1:T(8,128)} %param.28) | copy-start | bytes 884740
  683.0 10.4 %copy-start.13 = (f32[768,96]{0,1:T(8,128)S(1)}, f32[768,96]{0,1:T(8,128)}, u32[]{:S(2)}) copy-start(f32[768,96]{0,1:T(8,128)} %get-tuple-element.140) | copy-start | bytes 884740
  683.1 10.4 %copy-start.14 = (f32[768,96]{0,1:T(8,128)S(1)}, f32[768,96]{0,1:T(8,128)}, u32[]{:S(2)}) copy-start(f32[768,96]{0,1:T(8,128)} %get-tuple-element.141) | copy-start | bytes 884740
Sparse Core Ops, SparseCore 0:
  10.8 41.4 all-gather.2
  72.5 80.3 reduce-scatter.10
  155.6 43.7 all-gather.4
  202.5 61.3 reduce-scatter.14
  275.6 67.7 reduce-scatter.12
  346.8 68.7 reduce-scatter.8
  418.7 182.2 all-reduce.4
where the time goes:
time: 716 us; the launch traced here: 707 us
  waiting for transfers between devices  272 us (38%)
  blocking collectives  151 us (21%)
  matrix products  118 us (16%)
  other arithmetic  75.5 us (11%)
  local copies, waits for them, and re-layouts  66.7 us (9%)
  between operations  23.3 us (3%)
    psum x1, waiting for transfers between devices, local(): lax.psum(partial_sum.astype(jnp.bfloat16), 'tensor').astype(jnp.float32)  182 us
    reduce_scatter x1, waiting for transfers between devices, local(): lax.psum_scatter(grad_widening, 'dp', scatter_dimension=0, tiled=True)  66.2 us
    psum x1, blocking collectives, local(): trust_norms = jnp.sqrt(lax.psum(local_sums, ('dp', 'tensor')))  42.7 us
    all_gather x1, blocking collectives, local(): lax.all_gather(master_inward.astype(jnp.bfloat16), 'dp', axis=1, tiled=True)  40.9 us
    unnamed x2, blocking collectives  37.6 us
    all_gather x1, blocking collectives, local(): lax.all_gather(master_outward.astype(jnp.bfloat16), 'dp', axis=1, tiled=T...  30 us
    unnamed x120, local copies, waits for them, and re-layouts  27 us
  transfers between devices with their start and end apart: 7, of which 5 were waited for; matrix products, arithmetic and copies ran while one was open for 28% of the time, Pallas kernels for 0%

commit v1 on v0

--- a/solution.py
+++ b/solution.py
@@ -87,7 +87,9 @@
     )
     share = rows_here // lax.axis_size("tensor")
     start = lax.axis_index("tensor") * share
-    total = lax.psum(partial_sum.astype(jnp.bfloat16), "tensor").astype(jnp.float32)
+    total = jnp.sum(lax.all_gather(partial_sum.astype(jnp.bfloat16), "tensor"), axis=0).astype(
+        jnp.float32
+    )
     mixed = lax.dynamic_slice_in_dim(floats_in, start, share, 0) + lax.dynamic_slice_in_dim(
         total, start, share, 0
     )

time: 716 us -> 691 us (0.965)
  waiting for transfers between devices: 272 us -> 228 us
  other arithmetic: 75.5 us -> 94.2 us
    psum x1, waiting for transfers between devices: 182 us -> 95 us  [local(): lax.psum(back_sum.astype(jnp.bfloat16), 'tensor').astype(jnp.float32)]
    all_gather x0 -> x1, waiting for transfers between devices: none -> 62.4 us  [local(): lax.all_gather(partial_sum.astype(jnp.bfloat16), 'tensor')]
    reduce_scatter x1, waiting for transfers between devices: 66.2 us -> 44.9 us  [local(): lax.psum_scatter(grad_widening, 'dp', scatter_dimension=0, tiled=True)]
    reduce_sum x0 -> x1, other arithmetic: none -> 17.5 us  [local(): jnp.sum(lax.all_gather(partial_sum.astype(jnp.bfloat16), 'tensor'), axis=0)]
    unnamed x120 -> x118, local copies, waits for them, and re-layouts: 27 us -> 24.8 us
  transfers between devices with their start and end apart: 7 -> 8, of which waited for: 5 -> 6; matrix products, arithmetic and copies ran while one was open for 28% -> 34% of each run, Pallas kernels for 0% -> 0%
where the time goes in v1:
time: 691 us; the launch traced here: 679 us
  waiting for transfers between devices  228 us (33%)
  blocking collectives  150 us (22%)
  matrix products  118 us (17%)
  other arithmetic  94.2 us (14%)
  local copies, waits for them, and re-layouts  64.6 us (9%)
  between operations  23.3 us (3%)
    psum x1, waiting for transfers between devices, local(): lax.psum(back_sum.astype(jnp.bfloat16), 'tensor').astype(jnp.float32)  95 us
    all_gather x1, waiting for transfers between devices, local(): lax.all_gather(partial_sum.astype(jnp.bfloat16), 'tensor')  62.4 us
    reduce_scatter x1, waiting for transfers between devices, local(): lax.psum_scatter(grad_widening, 'dp', scatter_dimension=0, tiled=True)  44.9 us
    psum x1, blocking collectives, local(): trust_norms = jnp.sqrt(lax.psum(local_sums, ('dp', 'tensor')))  41.2 us
    all_gather x1, blocking collectives, local(): lax.all_gather(master_inward.astype(jnp.bfloat16), 'dp', axis=1, tiled=True)  41 us
    unnamed x2, blocking collectives  37.8 us
    all_gather x1, blocking collectives, local(): lax.all_gather(master_outward.astype(jnp.bfloat16), 'dp', axis=1, tiled=T...  30 us
    unnamed x118, local copies, waits for them, and re-layouts  24.8 us
  transfers between devices with their start and end apart: 8, of which 6 were waited for; matrix products, arithmetic and copies ran while one was open for 34% of the time, Pallas kernels for 0%

profile of v1, /device:TPU:10, one launch (start us, length us, event | category | flops | bytes accessed | tf_op | source)
XLA Modules:
  0.0 678.6 jit_solution(14191105578418812492)
XLA Ops:
  7.3 1.6 convert_element_type.119
  9.0 3.2 convert_reduce_fusion
  14.3 19.0 %all-reduce = bf16[768]{0:T(1024)(128)(2,1)S(1)} all-reduce(bf16[768]{0:T(1024)(128)(2,1)S(1)} %dynamic-update-slice), channel_id=1, replica_groups=mesh['dp'=8,'tensor'=4] {'dp'}, use_global_device_ids=true, to_apply=%add | all-reduce | flops 768 | bytes 3072
  33.3 4.1 multiply_reduce_fusion.1
  38.0 6.7 multiply_convert_fusion.2
  44.7 7.6 %all-gather.6.cloned.1.call-done = bf16[768,768]{1,0:T(8,128)(2,1)} async-done(((bf16[96,768]{1,0:T(8,128)(2,1)}), bf16[768,768]{1,0:T(8,128)(2,1)}) %all-gather.6.cloned.1.call-update) | async-done | bytes 1179664 | tf_op jit(solution)/shard_map/all_gather | solution.py:53
  52.3 6.5 fusion.63
  58.9 3.9 copy-done.46
  62.8 9.4 %fusion.47 = f32[768,768]{0,1:T(8,128)} fusion(bf16[3332,768]{1,0:T(8,128)(2,1)} %param.18, f32[3332,768]{1,0:T(8,128)S(1)} %fusion.63), kind=kOutput, calls=%fused_computation.110 | convolution fusion | flops 3953617920 | bytes 17713152 | tf_op jit(solution)/shard_map/rf,rd->fd/dot_general | solution.py:102
  73.0 41.0 %all_gather.22 = bf16[3,768,192]{2,0,1:T(4,128)(2,1)S(1)} all-gather(bf16[3,96,192]{2,0,1:T(4,128)(2,1)S(1)} %copy.122), channel_id=1, replica_groups=mesh['dp'=8,'tensor'=4] {'dp'}, dimensions={1}, use_global_device_ids=true | all-gather | bytes 995328 | tf_op jit(solution)/shard_map/all_gather | solution.py:51
  114.9 5.9 fusion.62
  121.2 1.4 fusion.59
  122.6 3.8 squeeze.7
  126.4 3.8 squeeze.8
  130.2 4.2 squeeze.6
  134.4 9.5 %multiply_reduce_fusion.2 = (f32[17,3,196]{2,1,0:T(4,128)S(1)}, f32[17,3,196,196]{2,3,1,0:T(8,128)}) fusion(bf16[17,196,3,64]{1,0,3,2:T(8,128)(2,1)} %squeeze.8, bf16[17,196,3,64]{1,0,3,2:T(8,128)(2,1)} %squeeze.7), kind=kOutput, calls=%fused_computation.31 | convolution fusion | flops 254688080 | bytes 10435824 | tf_op jit(solution)/shard_map/bqhd,bkhd->bhqk/dot_general | solution.py:73
  143.9 8.9 %reduce-scatter.11.cloned.1.call-done = f32[768,96]{0,1:T(8,128)} async-done(((f32[768,768]{0,1:T(8,128)}), f32[768,96]{0,1:T(8,128)}) %reduce-scatter.11.cloned.1.call-update) | async-done | bytes 294928 | tf_op jit(solution)/shard_map/reduce_scatter | solution.py:148
  152.8 2.6 multiply_reduce_fusion.4
  155.7 6.3 exponential_reduce_fusion
  162.6 2.1 fusion.24
  165.8 2.6 reshape.143
  168.4 6.0 convolution_bitcast_fusion
  174.6 30.0 %all_gather.23 = bf16[192,768]{0,1:T(8,128)(2,1)S(1)} all-gather(bf16[192,96]{0,1:T(8,128)(2,1)S(1)} %copy.129), channel_id=1, replica_groups=mesh['dp'=8,'tensor'=4] {'dp'}, dimensions={1}, use_global_device_ids=true | all-gather | bytes 331776 | tf_op jit(solution)/shard_map/all_gather | solution.py:52
  205.4 4.2 convolution_convert_fusion
  209.6 4.3 reshape.144
  213.9 12.6 %multiply_reduce_fusion = (f32[17,3,196]{2,1,0:T(4,128)S(1)}, f32[17,3,196,196]{2,3,1,0:T(8,128)}) fusion(f32[17,3,196,196]{2,3,1,0:T(8,128)} %get-tuple-element.168, f32[17,3,196]{2,1,0:T(4,128)S(1)} %log_add_fusion, bf16[17,196,3,64]{1,0,3,2:T(8,128)(2,1)} %copy-done.1, bf16[17,196,3,64]{1,0,3,2:T(8,128)(2,1)} %reshape.144), kind=kOutput, calls=%fused_computation.8 | convolution fusion | flops 258606512 | bytes 18312672 | tf_op jit(solution)/shard_map/bqhd,bkhd->bhqk/dot_general | solution.py:114
  226.6 5.9 multiply_convert_fusion
  232.6 1.8 fusion.27
  234.4 2.2 fusion.26
  236.5 3.3 fusion.25
  240.8 2.7 stack.74
  243.5 2.5 copy.134
  246.0 2.8 stack.73
  248.8 2.5 constant_dynamic-update-slice_fusion.2
  251.3 2.5 copy.140
  253.8 2.6 stack.75
  256.4 2.5 constant_dynamic-update-slice_fusion.1
  258.9 2.6 constant_dynamic-update-slice_fusion
  261.4 8.3 %fusion.21 = f32[3,768,192]{1,2,0:T(8,128)} fusion(bf16[3,3332,192]{1,2,0:T(8,128)(2,1)} %constant_dynamic-update-slice_fusion, bf16[3332,768]{1,0:T(8,128)(2,1)} %multiply_convert_fusion.2), kind=kOutput, calls=%fused_computation.44 | convolution fusion | flops 2947940352 | bytes 10725888 | tf_op jit(solution)/shard_map/rd,tre->tde/dot_general | solution.py:131
  269.7 2.9 copy.158
  272.7 2.8 reshape.158
  275.6 13.0 %fusion.15 = bf16[3332,768]{1,0:T(8,128)(2,1)S(1)} fusion(f32[3332,768]{1,0:T(8,128)} %copy-done.46, bf16[3332,768]{1,0:T(8,128)(2,1)} %param.18, bf16[768,768]{0,1:T(8,128)(2,1)} %all-gather.8.cloned.1.call-done), kind=kOutput, calls=%fused_computation.23 | convolution fusion | flops 3981766656 | bytes 21651456 | tf_op jit(solution)/shard_map/rd,fd->rf/dot_general | solution.py:101
  288.6 4.4 fusion.64
  293.0 6.5 fusion.16
  299.6 9.2 %fusion.65 = f32[768,768]{1,0:T(8,128)} fusion(bf16[3332,768]{1,0:T(8,128)(2,1)} %multiply_convert_fusion.2, bf16[3332,768]{1,0:T(8,128)(2,1)} %copy-done.45), kind=kOutput, calls=%fused_computation.123 | convolution fusion | flops 3930587136 | bytes 12595200 | tf_op jit(solution)/shard_map/rd,rf->df/dot_general | solution.py:105
  308.9 9.1 %fusion.48 = f32[3332,768]{1,0:T(8,128)S(1)} fusion(bf16[768,768]{0,1:T(8,128)(2,1)S(1)} %copy-done.44, f32[3332,768]{1,0:T(8,128)} %copy-done.46), kind=kOutput, calls=%fused_computation.111 | convolution fusion | flops 3953617920 | bytes 21651456 | tf_op jit(solution)/shard_map/dot_general | solution.py:85
  318.0 4.0 fusion.18
  323.1 7.2 %convert_element_type.108 = f32[3332,768]{1,0:T(8,128)} convert(bf16[3332,768]{1,0:T(8,128)(2,1)} %param.17) | non-fusion elementwise | flops 2558976 | bytes 15353856 | tf_op jit(solution)/shard_map/convert_element_type | solution.py:57
  333.1 1.4 maximum_bitcast_fusion.1
  334.5 9.0 %reduce-scatter.13.cloned.1.call-done = f32[96,576]{1,0:T(8,128)} async-done(((f32[768,576]{1,0:T(8,128)}), f32[96,576]{1,0:T(8,128)}) %reduce-scatter.13.cloned.1.call-update) | async-done | bytes 221200
  345.7 1.4 maximum_bitcast_fusion
  348.9 1.4 maximum_bitcast_fusion.3
  350.4 95.0 %all-reduce.4.cloned.1.call-done = bf16[3332,768]{1,0:T(8,128)(2,1)} async-done(((bf16[3332,768]{1,0:T(8,128)(2,1)}), bf16[3332,768]{1,0:T(8,128)(2,1)}) %all-reduce.4.cloned.1.call-update) | async-done | bytes 5117968 | tf_op jit(solution)/shard_map/psum | solution.py:135
  445.5 7.5 %fusion.8 = (f32[768]{0:T(1024)S(1)}, f32[3332]{0:T(1024)S(1)}, f32[3332]{0:T(1024)S(1)}) fusion(bf16[3332,768]{1,0:T(8,128)(2,1)} %all-reduce.4.cloned.1.call-done, bf16[3332,768]{1,0:T(8,128)(2,1)} %param.17, f32[3332]{0:T(1024)S(1)} %copy-done.32, f32[3332]{0:T(1024)S(1)} %copy-done.22, f32[768]{0:T(1024)S(1)} %copy-done.36), kind=kLoop, calls=%fused_computation.16 | loop fusion | flops 25582328 | bytes 10295360 | tf_op jit(solution)/shard_map/reduce_sum | solution.py:136
  452.9 18.9 %all-reduce.1 = f32[768]{0:T(1024)S(1)} all-reduce(f32[768]{0:T(1024)S(1)} %get-tuple-element.115), channel_id=7, replica_groups=mesh['dp'=8,'tensor'=4] {'dp'}, use_global_device_ids=true, to_apply=%region_23.0.clone | all-reduce | flops 768 | bytes 6144
  473.0 1.3 maximum_multiply_fusion
  474.3 44.9 %reduce-scatter.9.cloned.1.call-done = f32[96,768]{1,0:T(8,128)} async-done(((f32[768,768]{1,0:T(8,128)}), f32[96,768]{1,0:T(8,128)}) %reduce-scatter.9.cloned.1.call-update) | async-done | bytes 294928 | tf_op jit(solution)/shard_map/reduce_scatter | solution.py:147
  519.3 1.8 multiply_reduce_fusion.6
  521.1 1.4 maximum_bitcast_fusion.2
  522.7 11.5 %fusion.6 = bf16[3332,768]{1,0:T(8,128)(2,1)} fusion(bf16[3332,768]{1,0:T(8,128)(2,1)} %all-reduce.4.cloned.1.call-done, bf16[3332,768]{1,0:T(8,128)(2,1)} %param.18, bf16[3332,768]{1,0:T(8,128)(2,1)} %param.17, f32[3332]{0:T(1024)S(1)} %get-tuple-element.171, f32[3332]{0:T(1024)S(1)} %get-tuple-element.172, f32[768]{0:T(1024)S(1)} %copy-done.36, ...), kind=kLoop, calls=%fused_computation.14 | loop fusion | flops 30707712 | bytes 20528192 | tf_op jit(solution)/shard_map/convert_element_type | solution.py:143
  534.2 41.2 %psum.15 = f32[5,2]{0,1:T(2,128)S(1)} all-reduce(f32[5,2]{0,1:T(2,128)S(1)} %stack.96), channel_id=1, replica_groups=mesh['dp'=8,'tensor'=4] {'dp','tensor'}, use_global_device_ids=true, to_apply=%region_25.0 | all-reduce | flops 10 | bytes 80 | tf_op jit(solution)/shard_map/psum | solution.py:178
  587.7 62.4 %all-gather.10.cloned.1.call-done = bf16[4,3332,768]{2,1,0:T(8,128)(2,1)} async-done(((bf16[1,3332,768]{2,1,0:T(8,128)(2,1)}), bf16[4,3332,768]{2,1,0:T(8,128)(2,1)}) %all-gather.10.cloned.1.call-update) | async-done | bytes 20471824 | tf_op jit(solution)/shard_map/all_gather | solution.py:90
  650.1 17.5 %reduce_sum.168 = bf16[3332,768]{1,0:T(8,128)(2,1)} reduce(bf16[4,3332,768]{2,1,0:T(8,128)(2,1)} %all-gather.10.cloned.1.call-done, bf16[]{:T(256)} %constant.35.clone.1), dimensions={0}, to_apply=%region_4.0 | reduce | flops 7676928 | bytes 25589762 | tf_op jit(solution)/shard_map/reduce_sum | solution.py:90
  667.6 3.7 add_convert_fusion.1
  (159 shorter events, 22.7 us)
Async XLA Ops:
  7.2 5.6 copy-start.40
  7.2 5.0 copy-start.38
  7.2 45.1 %all-gather.6.cloned.1.call-start = ((), (), s32[]{:S(2)}) async-start(), calls=%async_computation.4 | async-start | bytes 1327104 | tf_op jit(solution)/shard_map/all_gather | solution.py:53
  8.9 143.8 %reduce-scatter.11.cloned.1.call-start = ((), (), s32[]{:S(2)}) async-start(), calls=%async_computation.8 | async-start | bytes 2654208 | tf_op jit(solution)/shard_map/reduce_scatter | solution.py:148
  33.3 4.1 copy-start.35
  33.3 4.1 copy-start.21
  37.4 0.6 copy-start.31
  58.9 3.9 copy-start.46
  62.8 9.5 %copy-start.9 = (f32[3,96,192]{2,1,0:T(8,128)S(1)}, f32[3,96,192]{2,1,0:T(8,128)}, u32[]{:S(2)}) copy-start(f32[3,96,192]{2,1,0:T(8,128)} %param.19) | copy-start | bytes 663556
  72.2 203.4 %all-gather.8.cloned.1.call-start = ((), (), s32[]{:S(2)}) async-start(), calls=%async_computation.5 | async-start | bytes 1327104 | tf_op jit(solution)/shard_map/all_gather | solution.py:54
  114.9 5.9 copy-start.17
  134.3 27.7 %copy-start.1 = (bf16[17,196,3,64]{1,0,3,2:T(8,128)(2,1)}, bf16[17,196,3,64]{1,0,3,2:T(8,128)(2,1)S(1)}, u32[]{:S(2)}) copy-start(bf16[17,196,3,64]{1,0,3,2:T(8,128)(2,1)S(1)} %squeeze.6) | copy-start | bytes 3838468
  134.4 18.4 %copy-start.11 = (f32[768,96]{0,1:T(8,128)S(1)}, f32[768,96]{0,1:T(8,128)}, u32[]{:S(2)}) copy-start(f32[768,96]{0,1:T(8,128)} %param.28) | copy-start | bytes 884740
  134.4 18.4 %copy-start.25 = (f32[768,96]{0,1:T(8,128)S(1)}, f32[768,96]{0,1:T(8,128)}, u32[]{:S(2)}) copy-start(f32[768,96]{0,1:T(8,128)} %param.29) | copy-start | bytes 884740
  134.4 18.4 %copy-start.26 = (f32[768,96]{0,1:T(8,128)S(1)}, f32[768,96]{0,1:T(8,128)}, u32[]{:S(2)}) copy-start(f32[768,96]{0,1:T(8,128)} %param.30) | copy-start | bytes 884740
  155.4 176.0 %reduce-scatter.15.cloned.1.call-start = ((), (), s32[]{:S(2)}) async-start(), calls=%async_computation.11 | async-start | bytes 884736
  155.6 6.9 %copy-start = (f32[17,3,196,196]{2,3,1,0:T(8,128)S(1)}, f32[17,3,196,196]{2,3,1,0:T(8,128)}, u32[]{:S(2)}) copy-start(f32[17,3,196,196]{2,3,1,0:T(8,128)} %get-tuple-element.168) | copy-start | bytes 23510596
  168.4 6.1 copy-start.19
  174.4 169.2 %reduce-scatter.13.cloned.1.call-start = ((), (), s32[]{:S(2)}) async-start(), calls=%async_computation.10 | async-start | bytes 2211840
  204.6 0.7 copy-start.6
  209.6 17.0 %slice-start = ((s8[10444800]{0:T(1024)(128)(4,1)}), s8[2056192]{0:T(1024)(128)(4,1)S(1)}, s32[]{:S(2)}) async-start(s8[10444800]{0:T(1024)(128)(4,1)} %bitcast.97), calls=%async_computation.12 | async-start | bytes 4112384
  213.9 12.7 %slice-start.1 = ((s8[10444800]{0:T(1024)(128)(4,1)}), s8[4194304]{0:T(1024)(128)(4,1)S(1)}, s32[]{:S(2)}) async-start(s8[10444800]{0:T(1024)(128)(4,1)} %bitcast.97), calls=%async_computation.13 | async-start | bytes 8388608
  213.9 12.7 %slice-start.2 = ((s8[10444800]{0:T(1024)(128)(4,1)}), s8[4194304]{0:T(1024)(128)(4,1)S(1)}, s32[]{:S(2)}) async-start(s8[10444800]{0:T(1024)(128)(4,1)} %bitcast.97), calls=%async_computation.14 | async-start | bytes 8388608
  226.6 5.9 copy-start.3
  232.5 1.8 copy-start.4
  234.4 2.2 copy-start.2
  275.5 13.1 %copy-start.43 = (bf16[768,768]{1,0:T(8,128)(2,1)S(1)}, bf16[768,768]{1,0:T(8,128)(2,1)}, u32[]{:S(2)}) copy-start(bf16[768,768]{1,0:T(8,128)(2,1)} %all-gather.6.cloned.1.call-done) | copy-start | bytes 3538948
  275.5 169.9 %all-reduce.4.cloned.1.call-start = ((), (), s32[]{:S(2)}) async-start(), calls=%async_computation.6 | async-start | bytes 10248192 | tf_op jit(solution)/shard_map/psum | solution.py:135
  288.6 4.4 copy-start.45
  288.6 4.4 copy-start.18
  288.6 4.4 copy-start.20
  299.5 9.4 %copy-start.44 = (bf16[768,768]{0,1:T(8,128)(2,1)S(1)}, bf16[768,768]{0,1:T(8,128)(2,1)}, u32[]{:S(2)}) copy-start(bf16[768,768]{0,1:T(8,128)(2,1)} %all-gather.8.cloned.1.call-done) | copy-start | bytes 3538948
  299.5 219.7 %reduce-scatter.9.cloned.1.call-start = ((), (), s32[]{:S(2)}) async-start(), calls=%async_computation.7 | async-start | bytes 2654208 | tf_op jit(solution)/shard_map/reduce_scatter | solution.py:147
  308.8 9.2 %copy-start.5 = (bf16[3332,192]{0,1:T(8,128)(2,1)S(1)}, bf16[3332,192]{0,1:T(8,128)(2,1)}, u32[]{:S(2)}) copy-start(bf16[3332,192]{0,1:T(8,128)(2,1)} %reshape.143) | copy-start | bytes 3838468
  308.9 9.2 %copy-start.7 = (bf16[192,768]{0,1:T(8,128)(2,1)S(1)}, bf16[192,768]{0,1:T(8,128)(2,1)}, u32[]{:S(2)}) copy-start(bf16[192,768]{0,1:T(8,128)(2,1)} %copy-done.6) | copy-start | bytes 884740
  308.9 341.2 %all-gather.10.cloned.1.call-start = ((), (), s32[]{:S(2)}) async-start(), calls=%async_computation.9 | async-start | bytes 25620480 | tf_op jit(solution)/shard_map/all_gather | solution.py:90
  322.0 1.0 copy-start.10
  323.1 7.3 %copy-start.27 = (f32[3,96,192]{2,1,0:T(8,128)S(1)}, f32[3,96,192]{2,1,0:T(8,128)}, u32[]{:S(2)}) copy-start(f32[3,96,192]{2,1,0:T(8,128)} %param.20) | copy-start | bytes 663556
  323.1 7.4 %copy-start.28 = (f32[3,96,192]{2,1,0:T(8,128)S(1)}, f32[3,96,192]{2,1,0:T(8,128)}, u32[]{:S(2)}) copy-start(f32[3,96,192]{2,1,0:T(8,128)} %param.21) | copy-start | bytes 663556
  323.1 9.3 %copy-start.33 = (f32[192,96]{1,0:T(8,128)S(1)}, f32[192,96]{1,0:T(8,128)}, u32[]{:S(2)}) copy-start(f32[192,96]{1,0:T(8,128)} %param.23) | copy-start | bytes 221188
  323.1 9.2 %copy-start.34 = (f32[192,96]{1,0:T(8,128)S(1)}, f32[192,96]{1,0:T(8,128)}, u32[]{:S(2)}) copy-start(f32[192,96]{1,0:T(8,128)} %param.24) | copy-start | bytes 221188
  330.4 115.1 %copy-start.22 = (f32[3332]{0:T(1024)S(1)}, f32[3332]{0:T(1024)}, u32[]{:S(2)}) copy-start(f32[3332]{0:T(1024)} %copy-done.21) | copy-start | bytes 39988
  330.4 115.1 %copy-start.32 = (f32[3332]{0:T(1024)S(1)}, f32[3332]{0:T(1024)}, u32[]{:S(2)}) copy-start(f32[3332]{0:T(1024)} %copy-done.31) | copy-start | bytes 39988
  330.4 115.1 %copy-start.36 = (f32[768]{0:T(1024)S(1)}, f32[768]{0:T(1024)}, u32[]{:S(2)}) copy-start(f32[768]{0:T(1024)} %copy-done.35) | copy-start | bytes 9220
  333.1 252.0 %copy-start.23 = (f32[192,96]{1,0:T(8,128)}, f32[192,96]{1,0:T(8,128)S(1)}, u32[]{:S(2)}) copy-start(f32[192,96]{1,0:T(8,128)S(1)} %get-tuple-element.142) | copy-start | bytes 221188
  333.1 252.0 %copy-start.24 = (f32[192,96]{1,0:T(8,128)}, f32[192,96]{1,0:T(8,128)S(1)}, u32[]{:S(2)}) copy-start(f32[192,96]{1,0:T(8,128)S(1)} %get-tuple-element.143) | copy-start | bytes 221188
  350.4 121.4 %copy-start.39 = (f32[96]{0:T(128)S(1)}, f32[96]{0:T(128)}, u32[]{:S(2)}) copy-start(f32[96]{0:T(128)} %param.31) | copy-start | bytes 1156
  350.4 121.4 %copy-start.41 = (f32[96]{0:T(128)S(1)}, f32[96]{0:T(128)}, u32[]{:S(2)}) copy-start(f32[96]{0:T(128)} %param.32) | copy-start | bytes 1156
  350.4 121.4 %copy-start.42 = (f32[96]{0:T(128)S(1)}, f32[96]{0:T(128)}, u32[]{:S(2)}) copy-start(f32[96]{0:T(128)} %param.33) | copy-start | bytes 1156
  350.4 168.9 %copy-start.8 = (f32[96,768]{1,0:T(8,128)S(1)}, f32[96,768]{1,0:T(8,128)}, u32[]{:S(2)}) copy-start(f32[96,768]{1,0:T(8,128)} %param.25) | copy-start | bytes 884740
  350.4 168.9 %copy-start.29 = (f32[96,768]{1,0:T(8,128)S(1)}, f32[96,768]{1,0:T(8,128)}, u32[]{:S(2)}) copy-start(f32[96,768]{1,0:T(8,128)} %param.26) | copy-start | bytes 884740
  350.4 168.9 %copy-start.30 = (f32[96,768]{1,0:T(8,128)S(1)}, f32[96,768]{1,0:T(8,128)}, u32[]{:S(2)}) copy-start(f32[96,768]{1,0:T(8,128)} %param.27) | copy-start | bytes 884740
  521.1 65.6 %copy-start.15 = (f32[96,768]{1,0:T(8,128)}, f32[96,768]{1,0:T(8,128)S(1)}, u32[]{:S(2)}) copy-start(f32[96,768]{1,0:T(8,128)S(1)} %get-tuple-element.140) | copy-start | bytes 884740
  521.1 65.6 %copy-start.16 = (f32[96,768]{1,0:T(8,128)}, f32[96,768]{1,0:T(8,128)S(1)}, u32[]{:S(2)}) copy-start(f32[96,768]{1,0:T(8,128)S(1)} %get-tuple-element.141) | copy-start | bytes 884740
  522.7 63.1 %copy-start.12 = (f32[768,96]{0,1:T(8,128)S(1)}, f32[768,96]{0,1:T(8,128)}, u32[]{:S(2)}) copy-start(f32[768,96]{0,1:T(8,128)} %param.28) | copy-start | bytes 884740
  522.7 63.1 %copy-start.13 = (f32[768,96]{0,1:T(8,128)S(1)}, f32[768,96]{0,1:T(8,128)}, u32[]{:S(2)}) copy-start(f32[768,96]{0,1:T(8,128)} %get-tuple-element.138) | copy-start | bytes 884740
  522.7 63.1 %copy-start.14 = (f32[768,96]{0,1:T(8,128)S(1)}, f32[768,96]{0,1:T(8,128)}, u32[]{:S(2)}) copy-start(f32[768,96]{0,1:T(8,128)} %get-tuple-element.139) | copy-start | bytes 884740
  575.4 92.3 %copy-start.37 = (f32[5,2]{0,1:T(2,128)}, f32[5,2]{0,1:T(2,128)S(1)}, u32[]{:S(2)}) copy-start(f32[5,2]{0,1:T(2,128)S(1)} %sqrt.23) | copy-start | bytes 124
Sparse Core Ops, SparseCore 0:
  10.8 41.4 all-gather.5
  72.3 80.4 reduce-scatter.10
  155.5 43.8 all-gather.7
  202.5 61.4 reduce-scatter.14
  275.6 67.8 reduce-scatter.12
  345.8 99.5 all-reduce.3
  448.9 70.2 reduce-scatter.8
  520.9 129.1 all-gather.9
